TPU v7x, 32 devices: a whole 2x2x4 slice. The times are simulated.
32 devices in a mesh: row: 16 (over z, y, x), col: 2 (over core).
Axes of the slice: x: 2, y: 2, z: 4, core: 2. Of those that a mesh axis runs over, the one named last changes fastest.
Arguments:
- block_ids: int32 [64, 8], replicated, may hold values from 0 to 383, as said below
- iface_counts: int32 [64], replicated, may hold values from 6 to 8
- inv_factor: bfloat16 [30208, 472], P(('row', 'col')), as said below
- coupling: bfloat16 [30208, 1024], P(('row', 'col')), may hold values from -0.375 to 0.375
- boundary_block: bfloat16 [24, 2048, 8, 256], P(None, 'row', None, 'col'), may hold values from -6 to 6
Outputs:
- schur: float32 [24, 2048, 8, 256], P(None, 'row', None, 'col')
Inputs may be any that keep to these rules, and one draw needn't show every extreme that they name: For j < 2, block_ids[s, j] is below 16, equals (s // 2 + j) modulo 2, and is the same for the 2 substructures that share s // 2. Apart from these shared first 2 ids, the ids of the 2 substructures that share s // 2 are distinct modulo 16. `inv_factor`: each substructure's block is lower triangular with a diagonal from 0.5 to 1.5.
All inputs are finite; a program needn't handle non-finite values.
Results may differ from a plain program's by a relative error of at most 0.00044.
Values sent between devices are 32-bit elements; how exact they have to be, the bound alone decides.
A program may use at most 64 MiB of HBM per device.

v0:
```python
import jax
import jax.numpy as jnp
from jax import lax
from jax.sharding import PartitionSpec as P

CS = 2


def passed_along(value, axis, steps):
    count = lax.axis_size(axis)
    pairs = [(source, (source + steps) % count) for source in range(count)]
    return lax.ppermute(value, axis, pairs)


def owner_table(ids, rows):
    return ((ids % rows)[None, :, :] == jnp.arange(rows, dtype=jnp.int32)[:, None, None]).astype(
        jnp.float32
    )


def dispatch(piece, ids, rows):
    return jnp.einsum(
        "psk,skab->pab", owner_table(ids, rows), piece, precision=lax.Precision.HIGHEST
    )


def settle(received, source_ids, column_slot, row_at, rows, cols, nq, cq):
    members = source_ids.shape[1]
    slot_count = source_ids.shape[2]
    single = (jnp.arange(members, dtype=jnp.int32)[:, None] == 0) | (
        jnp.arange(slot_count, dtype=jnp.int32)[None, :] >= CS
    )
    match = (source_ids % rows == row_at) & single[None]
    local_row = jnp.sum(jnp.where(match, source_ids // rows, 0), axis=(1, 2))
    local_col = source_ids[:, 0, column_slot] // cols
    place = (local_row[None, None, :] == jnp.arange(nq, dtype=jnp.int32)[:, None, None]) & (
        local_col[None, None, :] == jnp.arange(cq, dtype=jnp.int32)[None, :, None]
    )
    place = place.reshape(nq * cq, rows).astype(jnp.float32)
    return jnp.dot(place, received.reshape(rows, 128 * 128), precision=lax.Precision.HIGHEST)


def on_device(block_ids, iface_counts, inv_factor, coupling, boundary_block):
    rows = lax.axis_size("row")
    cols = lax.axis_size("col")
    row_at = lax.axis_index("row")
    col_at = lax.axis_index("col")
    slot_count = block_ids.shape[1]
    width = inv_factor.shape[1]
    members = inv_factor.shape[0] // width
    nq = boundary_block.shape[0]
    cq = boundary_block.shape[2]
    grid_ids = block_ids.reshape(rows, cols, members, slot_count)
    grid_counts = iface_counts.reshape(rows, cols, members)
    own_ids = lax.dynamic_index_in_dim(
        lax.dynamic_index_in_dim(grid_ids, row_at, 0, False), col_at, 0, False
    )
    own_count = lax.dynamic_index_in_dim(
        lax.dynamic_index_in_dim(grid_counts, row_at, 0, False), col_at, 0, False
    )
    factors = inv_factor.reshape(members, width, width)
    couples = coupling.reshape(members, width, slot_count * 128)
    tile_list = []
    for member in range(members):
        mixed = jnp.dot(
            factors[member], couples[member], preferred_element_type=jnp.float32
        ).astype(jnp.bfloat16)
        partial_value = lax.dot_general(
            mixed,
            mixed[:, : CS * 128],
            (((0,), (0,)), ((), ())),
            preferred_element_type=jnp.float32,
        )
        live = (jnp.arange(slot_count, dtype=jnp.int32) < own_count[member]).astype(jnp.float32)
        tile_list.append(
            partial_value.reshape(slot_count, 128, CS, 128) * live[:, None, None, None]
        )
    tiles = jnp.stack(tile_list, axis=0)
    sources = [
        lax.dynamic_index_in_dim(grid_ids, (col_at - slot) % cols, 1, False) for slot in range(CS)
    ]
    pieces = []
    outgoing = [dispatch(tiles[:, :, :, 0, :], own_ids, rows)]
    slot = 1
    moved = passed_along(tiles[:, :, :, slot, :], "col", slot)
    moved_ids = lax.dynamic_index_in_dim(sources[slot], row_at, 0, False)
    outgoing.append(dispatch(moved, moved_ids, rows))
    arrived = lax.all_to_all(
        jnp.stack(outgoing, axis=1), "row", split_axis=0, concat_axis=0, tiled=True
    )
    for slot in range(CS):
        pieces.append(arrived[:, slot])
    gathered = settle(pieces[0], sources[0], 0, row_at, rows, cols, nq, cq)
    slot = 1
    gathered = gathered + settle(pieces[slot], sources[slot], slot, row_at, rows, cols, nq, cq)
    gathered = gathered.reshape(nq, cq, 128, 128).transpose(0, 2, 1, 3)
    return boundary_block.astype(jnp.float32) - gathered


def solution(mesh):
    return jax.shard_map(
        on_device,
        mesh=mesh,
        in_specs=(
            P(),
            P(),
            P(("row", "col"), None),
            P(("row", "col"), None),
            P(None, "row", None, "col"),
        ),
        out_specs=P(None, "row", None, "col"),
        check_vma=False,
    )
```

profile of v0, /device:TPU:12, one launch (start us, length us, event | category | flops | bytes accessed | tf_op | source)
XLA Modules:
  0.0 87.4 jit_solution(4288207884399811646)
XLA Ops:
  0.0 0.0 copy-start.3
  0.0 0.0 copy-start.2
  0.0 2.2 %convolution_convert_fusion = bf16[472,1024]{1,0:T(8,128)(2,1)S(1)} fusion(bf16[944,1024]{1,0:T(8,128)(2,1)} %param.8, bf16[944,472]{1,0:T(8,128)(2,1)} %param.7), kind=kOutput, calls=%fused_computation.5 | convolution fusion | flops 456744960 | bytes 2416640 | tf_op jit(solution)/shard_map/dot_general | solution.py:65
  2.2 0.0 copy-done.3
  2.2 0.1 copy-done.2
  2.3 0.0 copy-start.1
  2.3 0.7 convolution_convert_fusion.1
  3.0 0.0 copy-done.1
  3.0 0.1 reshape.318
  3.1 0.6 fusion.49
  3.7 0.6 compare_convert_fusion.1
  4.4 0.6 compare_convert_fusion
  4.9 0.5 fusion.13
  5.4 0.5 reshape.319
  6.0 0.5 fusion.15
  6.5 1.5 %reshape.317 = f32[1,8,128,2,128]{4,3,2,1,0:T(2,128)} reshape(f32[1024,256]{1,0:T(8,128)S(1)} %fusion.15) | data formatting | bytes 2097152 | tf_op jit(solution)/shard_map/reshape | solution.py:76
  8.0 2.4 %copy_multiply_fusion = (f32[1,8,128,2,128]{4,1,0,2,3:T(8,128)S(1)}, f32[1,8,128,2,128]{4,1,0,2,3:T(8,128)S(1)}) fusion(f32[1,8,128,2,128]{4,3,2,1,0:T(2,128)S(1)} %reshape.319, f32[8]{0:T(128)S(1)} %compare_convert_fusion, f32[8]{0:T(128)S(1)} %compare_convert_fusion.1, f32[1,8,128,2,128]{4,3,2,1,0:T(2,128)} %reshape.317), kind=kLoop, calls=%fused_computation.18 | loop fusion | flops 524288 | bytes 4194368 | tf_op jit(solution)/shard_map/mul | solution.py:76
  10.4 0.0 copy-start
  10.4 0.1 fusion.8
  10.5 0.1 collective-permute-start
  10.6 0.5 copy-done
  11.1 0.1 copy.24
  11.2 0.7 convolution_bitcast_fusion.1
  11.9 1.5 %collective-permute-done = f32[2,8,128,128]{3,1,0,2:T(8,128)} collective-permute-done((f32[2,8,128,128]{3,1,0,2:T(8,128)S(1)}, f32[2,8,128,128]{3,1,0,2:T(8,128)}, u32[]{:S(2)}, u32[]{:S(2)}) %collective-permute-start) | collective-permute-done | bytes 1048608 | tf_op jit(solution)/shard_map/ppermute | solution.py:12
  13.4 1.9 %convolution_bitcast_fusion = f32[16,1,128,128]{3,0,2,1:T(8,128)S(1)} fusion(f32[2,8,128,128]{3,1,0,2:T(8,128)} %collective-permute-done, s32[2,8]{1,0:T(2,128)S(1)} %get-tuple-element.12), kind=kOutput, calls=%fused_computation.7 | convolution fusion | flops 50331904 | bytes 2097216 | tf_op jit(solution)/shard_map/psk,skab->pab/dot_general | solution.py:22
  15.3 0.1 pad_maximum_fusion
  15.4 2.0 %copy.28 = f32[16,2,128,128]{3,2,1,0:T(8,128)} copy(f32[16,2,128,128]{3,0,2,1:T(8,128)S(1)} %pad_maximum_fusion) | data formatting | bytes 4194304 | tf_op jit(solution)/shard_map/stack | solution.py:89
  17.4 7.2 %all-to-all-start = ((f32[16,2,128,128]{3,2,1,0:T(8,128)}), f32[16,2,128,128]{3,2,1,0:T(8,128)S(1)}, u32[]{:S(2)}, u32[]{:S(2)}) async-start(f32[16,2,128,128]{3,2,1,0:T(8,128)} %copy.28), calls=%async_computation | async-start | bytes 4194304 | tf_op jit(solution)/shard_map/all_to_all | solution.py:88
  24.6 0.1 copy.29
  24.7 0.1 copy.25
  24.7 0.1 broadcast_or_fusion
  24.8 0.1 fusion.30
  25.0 48.0 %all-to-all-done = f32[16,2,128,128]{3,2,1,0:T(8,128)S(1)} async-done(((f32[16,2,128,128]{3,2,1,0:T(8,128)}), f32[16,2,128,128]{3,2,1,0:T(8,128)S(1)}, u32[]{:S(2)}, u32[]{:S(2)}) %all-to-all-start) | async-done | bytes 2097184 | tf_op jit(solution)/shard_map/all_to_all | solution.py:88
  72.9 0.2 fusion.48
  73.1 0.0 slice-start
  73.1 0.0 slice-start.1
  73.1 5.1 %fusion.5 = f32[192,16384]{1,0:T(8,128)S(1)} fusion(f32[2,8,128,128]{3,2,1,0:T(8,128)S(1)} %bitcast.72, pred[8,16]{1,0:T(8,128)(4,1)S(1)} %iota_compare_fusion.5, pred[24,16]{1,0:T(8,128)(4,1)S(1)} %get-tuple-element.20), kind=kOutput, calls=%fused_computation.13 | convolution fusion | flops 603982848 | bytes 13632000 | tf_op jit(solution)/shard_map/dot_general | solution.py:40
  78.2 0.0 slice-done
  78.2 0.0 slice-done.1
  78.2 9.2 %bitcast_subtract_fusion = f32[24,128,8,128]{3,2,1,0:T(8,128)} fusion(bf16[24,128,8,128]{3,2,1,0:T(8,128)(2,1)S(1)} %bitcast.70, f32[192,16384]{1,0:T(8,128)S(1)} %fusion.5, f32[2,8,128,128]{3,2,1,0:T(8,128)S(1)} %bitcast.71, pred[8,16]{1,0:T(8,128)(4,1)S(1)} %iota_compare_fusion.4, pred[24,16]{1,0:T(8,128)(4,1)S(1)} %get-tuple-element.19), kind=kOutput, calls=%fused_computation.1 | convolution fusion | flops 613420032 | bytes 32506368 | tf_op jit(solution)/shard_map/dot_general | solution.py:40
  (10 shorter events, 0.1 us)
Async XLA Ops:
  0.0 2.2 %copy-start.3 = (bf16[944,472]{1,0:T(8,128)(2,1)S(1)}, bf16[944,472]{1,0:T(8,128)(2,1)}, u32[]{:S(2)}) copy-start(bf16[944,472]{1,0:T(8,128)(2,1)} %param.7) | copy-start | bytes 2673412
  0.0 2.3 %copy-start.2 = (bf16[944,1024]{1,0:T(8,128)(2,1)S(1)}, bf16[944,1024]{1,0:T(8,128)(2,1)}, u32[]{:S(2)}) copy-start(bf16[944,1024]{1,0:T(8,128)(2,1)} %param.8) | copy-start | bytes 5799940
  2.3 0.7 copy-start.1
  10.4 0.7 copy-start
  10.5 2.9 %collective-permute-start = (f32[2,8,128,128]{3,1,0,2:T(8,128)S(1)}, f32[2,8,128,128]{3,1,0,2:T(8,128)}, u32[]{:S(2)}, u32[]{:S(2)}) collective-permute-start(f32[2,8,128,128]{3,1,0,2:T(8,128)S(1)} %fusion.8), channel_id=1, source_target_pairs={{0,1},{1,0},{2,3},{3,2},{4,5},{5,4},{6,7},{7,6},{8,9},{9,8},{10,11... | collective-permute-start | bytes 3145736 | tf_op jit(solution)/shard_map/ppermute | solution.py:12
  17.4 55.5 %all-to-all-start = ((f32[16,2,128,128]{3,2,1,0:T(8,128)}), f32[16,2,128,128]{3,2,1,0:T(8,128)S(1)}, u32[]{:S(2)}, u32[]{:S(2)}) async-start(f32[16,2,128,128]{3,2,1,0:T(8,128)} %copy.28), calls=%async_computation | async-start | bytes 4194304 | tf_op jit(solution)/shard_map/all_to_all | solution.py:88
  73.1 5.1 %slice-start = ((s8[6291456]{0:T(1024)(128)(4,1)}), s8[4194304]{0:T(1024)(128)(4,1)S(1)}, s32[]{:S(2)}) async-start(s8[6291456]{0:T(1024)(128)(4,1)} %bitcast.69), calls=%async_computation.1 | async-start | bytes 8388608
  73.1 5.1 %slice-start.1 = ((s8[6291456]{0:T(1024)(128)(4,1)}), s8[2097152]{0:T(1024)(128)(4,1)S(1)}, s32[]{:S(2)}) async-start(s8[6291456]{0:T(1024)(128)(4,1)} %bitcast.69), calls=%async_computation.2 | async-start | bytes 4194304
where the time goes:
time: 87.7 us; the launch traced here: 87.4 us
  waiting for transfers between devices  49.4 us (56%)
  matrix products  20.7 us (24%)
  starting transfers between devices  7.24 us (8%)
  local copies, waits for them, and re-layouts  5.72 us (7%)
  other arithmetic  4.08 us (5%)
    all_to_all x1, waiting for transfers between devices, on_device(): lax.all_to_all(jnp.stack(outgoing, axis=1), 'row', split_axis=0, concat_a...  48 us
    dot_general x2, matrix products, settle(): jnp.dot(place, received.reshape(rows, 128 * 128), precision=lax.Precision...  14.3 us
    all_to_all x1, starting transfers between devices, on_device(): lax.all_to_all(jnp.stack(outgoing, axis=1), 'row', split_axis=0, concat_a...  7.17 us
    dot_general x2, matrix products, on_device(): jnp.dot(factors[member], couples[member], preferred_element_type=jnp.floa...  2.85 us
    dot_general x2, matrix products, dispatch(): jnp.einsum('psk,skab->pab', owner_table(ids, rows), piece, precision=lax....  2.6 us
    mul x1, other arithmetic, on_device(): partial_value.reshape(slot_count, 128, CS, 128) * live[:, None, None, None]  2.44 us
    reshape x2, local copies, waits for them, and re-layouts, on_device(): partial_value.reshape(slot_count, 128, CS, 128) * live[:, None, None, None]  2.03 us
    another operation x1, local copies, waits for them, and re-layouts, on_device(): jnp.stack(outgoing, axis=1)  1.96 us
  transfers between devices with their start and end apart: 2, of which 2 were waited for; matrix products, arithmetic and copies ran while one was open for 1% of the time, Pallas kernels for 0%

commit v1 on v0

v1 whole, which is shorter than its diff:
```python
import functools

import jax
import jax.numpy as jnp
from jax import lax
from jax.experimental import pallas as pl
from jax.experimental.pallas import tpu as pltpu
from jax.sharding import PartitionSpec as P

CS = 2
MESH = pl.DeviceIdType.MESH


def exchange_kernel(
    rows, cols, members, slots, width, nq, cq,
    ids_ref, counts_ref, w_ref, k_ref,
    recv_ref, place_ref,
    y_ref, p_ref, send_ref, send_sem, recv_sem,
):
    row_at = lax.axis_index("row")
    col_at = lax.axis_index("col")
    half = rows // 2
    side = row_at // half

    barrier = pltpu.get_barrier_semaphore()
    for r in range(1, rows):
        other = lax.rem(row_at + r, rows)
        pl.semaphore_signal(barrier, inc=1, device_id=(other, col_at), device_id_type=MESH)
    for r in range(rows):
        for j in range(1, CS):
            pl.semaphore_signal(
                barrier, inc=1, device_id=(r, lax.rem(col_at + j, cols)), device_id_type=MESH
            )
            if cols > 2:
                pl.semaphore_signal(
                    barrier, inc=1, device_id=(r, lax.rem(col_at + cols - j, cols)),
                    device_id_type=MESH,
                )

    own = (row_at * cols + col_at) * members
    for m in range(members):
        for n in range(0, slots * 128, 256):
            y_ref[m, :, n : n + 256] = jnp.dot(
                w_ref[m], k_ref[m, :, n : n + 256], preferred_element_type=jnp.float32
            ).astype(jnp.bfloat16)
        for n in range(0, slots, 2):
            part = lax.dot_general(
                y_ref[m, :, n * 128 : n * 128 + 256],
                y_ref[m, :, 0 : CS * 128],
                (((0,), (0,)), ((), ())),
                preferred_element_type=jnp.float32,
            )
            for d in range(2):
                for j in range(CS):
                    p_ref[m * slots + n + d, j] = part[
                        d * 128 : (d + 1) * 128, j * 128 : (j + 1) * 128
                    ]

    targets = []
    for i in range(half):
        targets.append((1 - side) * half + lax.rem(row_at + i, half))
        targets.append(side * half + lax.rem(row_at + i + 1, half))

    partners = (rows - 1) + (CS - 1) * rows * (2 if cols > 2 else 1)
    copies = []
    pending = []
    for i, target in enumerate(targets):
        picks = []
        for m in range(members):
            k, weight = jnp.int32(0), jnp.float32(0.0)
            count = counts_ref[own + m]
            for kk in range(slots):
                hit = (lax.rem(ids_ref[kk, own + m], rows) == target) & (kk < count)
                k = jnp.where(hit, jnp.int32(kk), k)
                weight = jnp.where(hit, jnp.float32(1.0), weight)
            picks.append((m * slots + k, weight))
        if i == 1:
            pl.semaphore_wait(barrier, partners)
        for j in range(CS):
            total = p_ref[picks[0][0], j] * picks[0][1]
            for k, weight in picks[1:]:
                total = total + p_ref[k, j] * weight
            send_ref[j * rows + i] = total
            if j == 0 and i == rows - 1:
                pending.append(
                    pltpu.make_async_copy(
                        send_ref.at[j * rows + i], recv_ref.at[j * rows + row_at], recv_sem
                    )
                )
            else:
                copy = pltpu.make_async_remote_copy(
                    src_ref=send_ref.at[j * rows + i],
                    dst_ref=recv_ref.at[j * rows + row_at],
                    send_sem=send_sem,
                    recv_sem=recv_sem,
                    device_id=(target, lax.rem(col_at + j, cols)),
                    device_id_type=MESH,
                )
                pending.append(copy)
        if i >= 1:
            while len(pending) > CS:
                pending.pop(0).start()
    while pending:
        pending.pop(0).start()

    wide = place_ref.shape[1]
    sources = CS * rows
    cell_iota = lax.broadcasted_iota(jnp.int32, (nq * cq, wide), 0)
    lane_iota = lax.broadcasted_iota(jnp.int32, (nq * cq, wide), 1)

    def add_source(r, cells):
        for j in range(CS):
            first = (r * cols + lax.rem(col_at + cols - j, cols)) * members
            cell = jnp.int32(-1)
            column = lax.div(ids_ref[j, first], cols)
            for m in range(members):
                for kk in range(slots):
                    if m > 0 and kk < CS:
                        continue
                    ident = ids_ref[kk, first + m]
                    cell = jnp.where(
                        lax.rem(ident, rows) == row_at,
                        lax.div(ident, rows) * cq + column,
                        cell,
                    )
            lane = lane_iota - (j * rows + r)
            cells = jnp.where((lane == 0) | (lane == sources), cell, cells)
        return cells

    cells = lax.fori_loop(0, rows, add_source, jnp.full((nq * cq, wide), -1, jnp.int32))
    place_ref[...] = (cells == cell_iota).astype(jnp.float32).astype(jnp.bfloat16)

    pltpu.make_async_copy(recv_ref, recv_ref, recv_sem).wait()
    sent = send_ref.at[pl.ds(0, CS * rows - 1)]
    pltpu.make_async_copy(sent, sent, send_sem).wait()


def place_kernel(sources, place_ref, recv_ref, boundary_ref, out_ref):
    place = place_ref[...]
    nq, height, cq, _ = out_ref.shape
    for a in range(height):
        tile_rows = recv_ref[:, a, :]
        high = tile_rows.astype(jnp.bfloat16)
        low = (tile_rows - high.astype(jnp.float32)).astype(jnp.bfloat16)
        both = jnp.concatenate([high, low], axis=0)
        total = jnp.dot(place, both, preferred_element_type=jnp.float32)
        out_ref[:, a] = boundary_ref[:, a].astype(jnp.float32) - total.reshape(nq, cq, 128)


def on_device(rows, cols, block_ids, iface_counts, inv_factor, coupling, boundary_block):
    slots = block_ids.shape[1]
    width = inv_factor.shape[1]
    members = inv_factor.shape[0] // width
    nq, tall, cq, _ = boundary_block.shape
    sources = CS * rows
    received, place = pl.pallas_call(
        functools.partial(exchange_kernel, rows, cols, members, slots, width, nq, cq),
        out_shape=(
            jax.ShapeDtypeStruct((sources, 128, 128), jnp.float32),
            jax.ShapeDtypeStruct((nq * cq, 2 * sources), jnp.bfloat16),
        ),
        in_specs=[
            pl.BlockSpec(memory_space=pltpu.SMEM),
            pl.BlockSpec(memory_space=pltpu.SMEM),
            pl.BlockSpec(memory_space=pltpu.VMEM),
            pl.BlockSpec(memory_space=pltpu.VMEM),
        ],
        out_specs=(
            pl.BlockSpec(memory_space=pl.ANY),
            pl.BlockSpec(memory_space=pltpu.VMEM),
        ),
        scratch_shapes=[
            pltpu.VMEM((members, width, slots * 128), jnp.bfloat16),
            pltpu.VMEM((members * slots, CS, 128, 128), jnp.float32),
            pltpu.VMEM((sources, 128, 128), jnp.float32),
            pltpu.SemaphoreType.DMA,
            pltpu.SemaphoreType.DMA,
        ],
        compiler_params=pltpu.CompilerParams(collective_id=0, has_side_effects=True),
        name="exchange",
    )(
        block_ids.T,
        iface_counts,
        inv_factor.reshape(members, width, width),
        coupling.reshape(members, width, slots * 128),
    )
    step = 16
    return pl.pallas_call(
        functools.partial(place_kernel, sources),
        grid=(tall // step,),
        out_shape=jax.ShapeDtypeStruct(boundary_block.shape, jnp.float32),
        in_specs=[
            pl.BlockSpec((nq * cq, 2 * sources), lambda i: (0, 0)),
            pl.BlockSpec((sources, step, 128), lambda i: (0, i, 0)),
            pl.BlockSpec((nq, step, cq, 128), lambda i: (0, i, 0, 0)),
        ],
        out_specs=pl.BlockSpec((nq, step, cq, 128), lambda i: (0, i, 0, 0)),
        name="placing",
    )(place, received, boundary_block)


def solution(mesh):
    return jax.shard_map(
        functools.partial(on_device, mesh.shape["row"], mesh.shape["col"]),
        mesh=mesh,
        in_specs=(
            P(),
            P(),
            P(("row", "col"), None),
            P(("row", "col"), None),
            P(None, "row", None, "col"),
        ),
        out_specs=P(None, "row", None, "col"),
        check_vma=False,
    )
```

time: 87.7 us -> 69.5 us (0.79)
  the two profiles are of different devices: /device:TPU:12 before, /device:TPU:1 now
where the time goes in v1:
time: 69.5 us; the launch traced here: 68.3 us
  Pallas kernels  68.3 us (98%)
    pallas_call x1, Pallas kernels, on_device(): pl.pallas_call(functools.partial(exchange_kernel, rows, cols, members, sl...  55.7 us
    pallas_call x1, Pallas kernels, on_device(): pl.pallas_call(functools.partial(place_kernel, sources), grid=(tall // st...  12.6 us

profile of v1, /device:TPU:1, one launch (start us, length us, event | category | flops | bytes accessed | tf_op | source)
XLA Modules:
  0.0 68.3 jit_solution(4805579896469305090)
XLA Ops:
  0.0 55.7 %exchange.1 = (f32[32,128,128]{2,1,0:T(8,128)}, bf16[192,64]{1,0:T(8,128)(2,1)}) custom-call(s32[8,64]{1,0:T(8,128)} %bitcast.5, s32[64]{0:T(128)} %counts_ref.1, bf16[2,472,472]{2,1,0:T(8,128)(2,1)} %bitcast.4, bf16[2,472,1024]{2,1,0:T(8,128)(2,1)} %bitcast.3), custom_call_target="tpu_custom_call" | custom-call | tf_op jit(solution)/shard_map/exchange/pallas_call | solution.py:156
  55.7 12.6 %placing.1 = f32[24,128,8,128]{3,2,1,0:T(8,128)} custom-call(bf16[192,64]{1,0:T(8,128)(2,1)} %get-tuple-element.7.place_ref, f32[32,128,128]{2,1,0:T(8,128)} %get-tuple-element.8.recv_ref, bf16[24,128,8,128]{3,2,1,0:T(8,128)(2,1)} %boundary_ref.1), custom_call_target="tpu_custom_call" | custom-call | tf_op jit(solution)/shard_map/placing/pallas_call | solution.py:188

commit v2 on v1

v2 whole, which is shorter than its diff:
```python
import functools

import jax
import jax.numpy as jnp
from jax import lax
from jax.experimental import pallas as pl
from jax.experimental.pallas import tpu as pltpu
from jax.sharding import PartitionSpec as P

CS = 2
MESH = pl.DeviceIdType.MESH


def exchange_kernel(
    rows, cols, members, slots, width, nq, cq,
    pieces,
    ids_ref, counts_ref, factor_ref, couple_ref, boundary_ref,
    out_ref,
    w_ref, k_ref, y_ref, p_ref, send_ref, recv_ref, given_ref, place_ref,
    load_sem, send_sem, recv_sem, given_sem,
):
    row_at = lax.axis_index("row")
    col_at = lax.axis_index("col")
    half = rows // 2
    side = row_at // half

    loads = []
    for m in range(members):
        loads.append(
            (
                pltpu.make_async_copy(factor_ref.at[m], w_ref.at[m], load_sem.at[2 * m]),
                pltpu.make_async_copy(couple_ref.at[m], k_ref.at[m], load_sem.at[2 * m + 1]),
            )
        )
        for load in loads[-1]:
            load.start()

    barrier = pltpu.get_barrier_semaphore()
    for r in range(1, rows):
        other = lax.rem(row_at + r, rows)
        pl.semaphore_signal(barrier, inc=1, device_id=(other, col_at), device_id_type=MESH)
    for r in range(rows):
        for j in range(1, CS):
            pl.semaphore_signal(
                barrier, inc=1, device_id=(r, lax.rem(col_at + j, cols)), device_id_type=MESH
            )
            if cols > 2:
                pl.semaphore_signal(
                    barrier, inc=1, device_id=(r, lax.rem(col_at + cols - j, cols)),
                    device_id_type=MESH,
                )

    given = pltpu.make_async_copy(boundary_ref, given_ref, given_sem)
    given.start()

    own = (row_at * cols + col_at) * members
    for m in range(members):
        for load in loads[m]:
            load.wait()
        for n in range(0, slots * 128, 256):
            y_ref[m, :, n : n + 256] = jnp.dot(
                w_ref[m], k_ref[m, :, n : n + 256], preferred_element_type=jnp.float32
            ).astype(jnp.bfloat16)
        for n in range(0, slots, 2):
            part = lax.dot_general(
                y_ref[m, :, n * 128 : n * 128 + 256],
                y_ref[m, :, 0 : CS * 128],
                (((0,), (0,)), ((), ())),
                preferred_element_type=jnp.float32,
            )
            for d in range(2):
                for j in range(CS):
                    p_ref[m * slots + n + d, j] = part[
                        d * 128 : (d + 1) * 128, j * 128 : (j + 1) * 128
                    ]

    targets = []
    for i in range(half):
        targets.append((1 - side) * half + lax.rem(row_at + i, half))
        targets.append(side * half + lax.rem(row_at + i + 1, half))

    partners = (rows - 1) + (CS - 1) * rows * (2 if cols > 2 else 1)
    def route(i, target, j, piece):
        start, height = pieces[piece]
        src = send_ref.at[pl.ds((j * rows + i) * 128 + start, height)]
        dst = recv_ref.at[pl.ds((j * rows + row_at) * 128 + start, height)]
        if j == 0 and i == rows - 1:
            return pltpu.make_async_copy(src, dst, recv_sem.at[piece])
        return pltpu.make_async_remote_copy(
            src_ref=src,
            dst_ref=dst,
            send_sem=send_sem,
            recv_sem=recv_sem.at[piece],
            device_id=(target, lax.rem(col_at + j, cols)),
            device_id_type=MESH,
        )

    for i, target in enumerate(targets):
        picks = []
        for m in range(members):
            k, weight = jnp.int32(0), jnp.float32(0.0)
            count = counts_ref[own + m]
            for kk in range(slots):
                hit = (lax.rem(ids_ref[kk, own + m], rows) == target) & (kk < count)
                k = jnp.where(hit, jnp.int32(kk), k)
                weight = jnp.where(hit, jnp.float32(1.0), weight)
            picks.append((m * slots + k, weight))
        for j in range(CS):
            total = p_ref[picks[0][0], j] * picks[0][1]
            for k, weight in picks[1:]:
                total = total + p_ref[k, j] * weight
            send_ref[(j * rows + i) * 128 : (j * rows + i + 1) * 128] = total
        if i == 1:
            pl.semaphore_wait(barrier, partners)
        if i >= 1:
            for j in range(CS):
                route(i - 1, targets[i - 1], j, 0).start()
    for j in range(CS):
        route(rows - 1, targets[-1], j, 0).start()
    for piece in range(1, len(pieces)):
        for i, target in enumerate(targets):
            for j in range(CS):
                route(i, target, j, piece).start()

    wide = place_ref.shape[1]
    sources = CS * rows
    cell_iota = lax.broadcasted_iota(jnp.int32, (nq * cq, wide), 0)
    lane_iota = lax.broadcasted_iota(jnp.int32, (nq * cq, wide), 1)

    def add_source(r, cells):
        for j in range(CS):
            first = (r * cols + lax.rem(col_at + cols - j, cols)) * members
            cell = jnp.int32(-1)
            column = lax.div(ids_ref[j, first], cols)
            for m in range(members):
                for kk in range(slots):
                    if m > 0 and kk < CS:
                        continue
                    ident = ids_ref[kk, first + m]
                    cell = jnp.where(
                        lax.rem(ident, rows) == row_at,
                        lax.div(ident, rows) * cq + column,
                        cell,
                    )
            lane = lane_iota - (j * rows + r)
            cells = jnp.where((lane == 0) | (lane == sources), cell, cells)
        return cells

    cells = lax.fori_loop(0, rows, add_source, jnp.full((nq * cq, wide), -1, jnp.int32))
    place_ref[...] = (cells == cell_iota).astype(jnp.float32).astype(jnp.bfloat16)

    given.wait()
    place = place_ref[...]
    for piece, (start, height) in enumerate(pieces):
        arrived = recv_ref.at[pl.ds(0, sources * height)]
        pltpu.make_async_copy(arrived, arrived, recv_sem.at[piece]).wait()

        def place_rows(step, carry):
            halves = []
            first = start + step * 4
            for a in range(4):
                line = recv_ref[pl.ds(first + a, sources, stride=128), :]
                high = line.astype(jnp.bfloat16)
                low = (line - high.astype(jnp.float32)).astype(jnp.bfloat16)
                halves.append(jnp.concatenate([high, low], axis=0))
            for a in range(0, 4, 2):
                both = jnp.concatenate(halves[a : a + 2], axis=1)
                total = jnp.dot(place, both, preferred_element_type=jnp.float32)
                for d in range(2):
                    out_ref[:, first + a + d] = given_ref[:, first + a + d].astype(
                        jnp.float32
                    ) - total[:, d * 128 : (d + 1) * 128].reshape(nq, cq, 128)
            return carry

        lax.fori_loop(0, height // 4, place_rows, 0)
    sent = send_ref.at[pl.ds(0, (sources - 1) * 128)]
    pltpu.make_async_copy(sent, sent, send_sem).wait()


def write_kernel(result_ref, out_ref, sem):
    copies = []
    count = 8
    height = result_ref.shape[0] // count
    for i in range(count):
        part = pl.ds(i * height, height)
        copies.append(pltpu.make_async_copy(result_ref.at[part], out_ref.at[part], sem))
        copies[-1].start()
    pltpu.make_async_copy(result_ref, out_ref, sem).wait()


def kept(value):
    return pltpu.with_memory_space_constraint(value, pltpu.HBM)


def on_device(rows, cols, block_ids, iface_counts, inv_factor, coupling, boundary_block):
    slots = block_ids.shape[1]
    width = inv_factor.shape[1]
    members = inv_factor.shape[0] // width
    nq, tall, cq, _ = boundary_block.shape
    sources = CS * rows
    pieces = ((0, 96), (96, 32))
    result = pl.pallas_call(
        functools.partial(exchange_kernel, rows, cols, members, slots, width, nq, cq, pieces),
        out_shape=jax.ShapeDtypeStruct(boundary_block.shape, jnp.float32),
        in_specs=[
            pl.BlockSpec(memory_space=pltpu.SMEM),
            pl.BlockSpec(memory_space=pltpu.SMEM),
            pl.BlockSpec(memory_space=pltpu.HBM),
            pl.BlockSpec(memory_space=pltpu.HBM),
            pl.BlockSpec(memory_space=pltpu.HBM),
        ],
        out_specs=pl.BlockSpec(memory_space=pltpu.VMEM),
        scratch_shapes=[
            pltpu.VMEM((members, width, width), jnp.bfloat16),
            pltpu.VMEM((members, width, slots * 128), jnp.bfloat16),
            pltpu.VMEM((members, width, slots * 128), jnp.bfloat16),
            pltpu.VMEM((members * slots, CS, 128, 128), jnp.float32),
            pltpu.VMEM((sources * 128, 128), jnp.float32),
            pltpu.VMEM((sources * 128, 128), jnp.float32),
            pltpu.VMEM(boundary_block.shape, jnp.bfloat16),
            pltpu.VMEM((nq * cq, 2 * sources), jnp.bfloat16),
            pltpu.SemaphoreType.DMA((2 * members,)),
            pltpu.SemaphoreType.DMA,
            pltpu.SemaphoreType.DMA((len(pieces),)),
            pltpu.SemaphoreType.DMA,
        ],
        compiler_params=pltpu.CompilerParams(
            collective_id=0, has_side_effects=True, vmem_limit_bytes=32 * 1024 * 1024
        ),
        name="exchange",
    )(
        kept(block_ids.T),
        kept(iface_counts),
        kept(inv_factor.reshape(members, width, width)),
        kept(coupling.reshape(members, width, slots * 128)),
        kept(boundary_block),
    )
    return pl.pallas_call(
        write_kernel,
        out_shape=jax.ShapeDtypeStruct(boundary_block.shape, jnp.float32),
        in_specs=[pl.BlockSpec(memory_space=pltpu.VMEM)],
        out_specs=pl.BlockSpec(memory_space=pltpu.HBM),
        scratch_shapes=[pltpu.SemaphoreType.DMA],
        compiler_params=pltpu.CompilerParams(vmem_limit_bytes=16 * 1024 * 1024),
        name="writing",
    )(result)


def solution(mesh):
    return jax.shard_map(
        functools.partial(on_device, mesh.shape["row"], mesh.shape["col"]),
        mesh=mesh,
        in_specs=(
            P(),
            P(),
            P(("row", "col"), None),
            P(("row", "col"), None),
            P(None, "row", None, "col"),
        ),
        out_specs=P(None, "row", None, "col"),
        check_vma=False,
    )
```

time: 69.5 us -> 61.5 us (0.88); the launches traced: 68.3 us -> 61.3 us
  Pallas kernels: 68.3 us -> 61.3 us
    pallas_call x1, Pallas kernels: 12.6 us -> 4.6 us  [on_device(): pl.pallas_call(write_kernel, out_shape=jax.ShapeDtypeStruct(boundary_bloc...]
    pallas_call x1, Pallas kernels: 55.7 us -> 56.7 us  [on_device(): pl.pallas_call(functools.partial(exchange_kernel, rows, cols, members, sl...]
where the time goes in v2:
time: 61.5 us; the launch traced here: 61.3 us
  Pallas kernels  61.3 us (100%)
    pallas_call x1, Pallas kernels, on_device(): pl.pallas_call(functools.partial(exchange_kernel, rows, cols, members, sl...  56.7 us
    pallas_call x1, Pallas kernels, on_device(): pl.pallas_call(write_kernel, out_shape=jax.ShapeDtypeStruct(boundary_bloc...  4.6 us

profile of v2, /device:TPU:1, one launch (start us, length us, event | category | flops | bytes accessed | tf_op | source)
XLA Modules:
  0.0 61.3 jit_solution(11488401679710799264)
XLA Ops:
  0.0 56.7 %exchange.1.result_ref = f32[24,128,8,128]{3,2,1,0:T(8,128)S(1)} custom-call(s32[8,64]{1,0:T(8,128)} %bitcast.5, s32[64]{0:T(128)} %counts_ref.1, bf16[2,472,472]{2,1,0:T(8,128)(2,1)} %bitcast.4, bf16[2,472,1024]{2,1,0:T(8,128)(2,1)} %bitcast.3, bf16[24,128,8,128]{3,2,1,0:T(8,128)(2,1)} %boundary_ref.1), custom_call_target="tpu_custom_call" | custom-call | tf_op jit(solution)/shard_map/exchange/pallas_call | solution.py:202
  56.7 4.6 %writing.1 = f32[24,128,8,128]{3,2,1,0:T(8,128)} custom-call(f32[24,128,8,128]{3,2,1,0:T(8,128)S(1)} %exchange.1.result_ref), custom_call_target="tpu_custom_call" | custom-call | tf_op jit(solution)/shard_map/writing/pallas_call | solution.py:238

commit v3 on v2

--- a/solution.py
+++ b/solution.py
@@ -53,14 +53,18 @@
     given = pltpu.make_async_copy(boundary_ref, given_ref, given_sem)
     given.start()
 
+    split = width // 2 // 128 * 128 + 128
     own = (row_at * cols + col_at) * members
     for m in range(members):
         for load in loads[m]:
             load.wait()
         for n in range(0, slots * 128, 256):
-            y_ref[m, :, n : n + 256] = jnp.dot(
-                w_ref[m], k_ref[m, :, n : n + 256], preferred_element_type=jnp.float32
-            ).astype(jnp.bfloat16)
+            for top, bottom in ((0, split), (split, width)):
+                y_ref[m, top:bottom, n : n + 256] = jnp.dot(
+                    w_ref[m, top:bottom, 0:bottom],
+                    k_ref[m, 0:bottom, n : n + 256],
+                    preferred_element_type=jnp.float32,
+                ).astype(jnp.bfloat16)
         for n in range(0, slots, 2):
             part = lax.dot_general(
                 y_ref[m, :, n * 128 : n * 128 + 256],
@@ -198,7 +202,7 @@
     members = inv_factor.shape[0] // width
     nq, tall, cq, _ = boundary_block.shape
     sources = CS * rows
-    pieces = ((0, 96), (96, 32))
+    pieces = ((0, 112), (112, 16))
     result = pl.pallas_call(
         functools.partial(exchange_kernel, rows, cols, members, slots, width, nq, cq, pieces),
         out_shape=jax.ShapeDtypeStruct(boundary_block.shape, jnp.float32),

time: 61.5 us -> 64.1 us (1.042)
  Pallas kernels: 61.3 us -> 64 us
    pallas_call x1, Pallas kernels: 56.7 us -> 59.4 us  [on_device(): pl.pallas_call(functools.partial(exchange_kernel, rows, cols, members, sl...]
where the time goes in v3:
time: 64.1 us; the launch traced here: 64 us
  Pallas kernels  64 us (100%)
    pallas_call x1, Pallas kernels, on_device(): pl.pallas_call(functools.partial(exchange_kernel, rows, cols, members, sl...  59.4 us
    pallas_call x1, Pallas kernels, on_device(): pl.pallas_call(write_kernel, out_shape=jax.ShapeDtypeStruct(boundary_bloc...  4.6 us

profile of v3, /device:TPU:1, one launch (start us, length us, event | category | flops | bytes accessed | tf_op | source)
XLA Modules:
  0.0 64.0 jit_solution(3711695923216256329)
XLA Ops:
  0.0 59.4 %exchange.1.result_ref = f32[24,128,8,128]{3,2,1,0:T(8,128)S(1)} custom-call(s32[8,64]{1,0:T(8,128)} %bitcast.5, s32[64]{0:T(128)} %counts_ref.1, bf16[2,472,472]{2,1,0:T(8,128)(2,1)} %bitcast.4, bf16[2,472,1024]{2,1,0:T(8,128)(2,1)} %bitcast.3, bf16[24,128,8,128]{3,2,1,0:T(8,128)(2,1)} %boundary_ref.1), custom_call_target="tpu_custom_call" | custom-call | tf_op jit(solution)/shard_map/exchange/pallas_call | solution.py:206
  59.4 4.6 %writing.1 = f32[24,128,8,128]{3,2,1,0:T(8,128)} custom-call(f32[24,128,8,128]{3,2,1,0:T(8,128)S(1)} %exchange.1.result_ref), custom_call_target="tpu_custom_call" | custom-call | tf_op jit(solution)/shard_map/writing/pallas_call | solution.py:242
